TPU v7x, 512 devices: a whole 4x8x8 slice. The times are simulated.
512 devices in a mesh: owner: 32 (over y, x), rows: 16 (over z, core).
Axes of the slice: x: 4, y: 8, z: 8, core: 2. Of those that a mesh axis runs over, the one named last changes fastest.
Arguments:
- w_down: float32 [64, 1408, 2048], P('owner', None, 'rows'), may hold values from -0.21875 to 0.21875
- router_weight: float32 [2048, 64], P('rows', 'owner'), may hold values from -0.125 to 0.125
- router_gain: float32 [2048], P('rows'), may hold values from 0.25 to 1.75
Outputs:
- serve_down: bfloat16 [64, 1408, 2048], P('owner')
- scale_down: float32 [64, 1408], P('owner')
- serve_router: bfloat16 [2048, 64], replicated
All inputs are finite; a program needn't handle non-finite values. Where the computation divides by a largest or mean magnitude, that divisor is 1e-20 or more.
Results may differ from a plain program's by a relative error of at most 0.001.
Values may be sent and summed in bfloat16 or wider, within the bound.
A program may use at most 128 MiB of HBM per device.

v0:
```python
import jax
import jax.numpy as jnp
from jax import lax
from jax.sharding import PartitionSpec as P


def sent_to_all(x, axis):
    copies = jnp.broadcast_to(x, (lax.axis_size(axis), *x.shape))
    return lax.all_to_all(copies, axis, split_axis=0, concat_axis=0, tiled=True)


def of_everyone(x, axis):
    everything = sent_to_all(x, axis)
    return jnp.max(everything, axis=0)


def laid_out(pieces, dim):
    pieces = jnp.moveaxis(pieces, 0, dim)
    lengths = pieces.shape
    return pieces.reshape(*lengths[:dim], lengths[dim] * lengths[dim + 1], *lengths[dim + 2 :])


def collect(x, axis, dim):
    return laid_out(sent_to_all(x, axis), dim)


def on_device(w_down, router_weight, router_gain):
    scale_down = of_everyone(jnp.max(jnp.abs(w_down), axis=2), "rows")
    narrow_down = (w_down / jnp.expand_dims(scale_down, 2)).astype(jnp.bfloat16)
    serve_down = lax.all_gather(narrow_down, "rows", axis=2, tiled=True)
    part_router = (router_weight * router_gain[:, None]).astype(jnp.bfloat16)
    row_router = lax.all_gather(part_router, "rows", axis=0, tiled=True)
    serve_router = collect(row_router, "owner", 1)
    return (serve_down, scale_down, serve_router)


def solution(mesh):
    placed = (P("owner", None, "rows"), P("rows", "owner"), P("rows"))
    return jax.shard_map(
        on_device,
        mesh=mesh,
        in_specs=placed,
        out_specs=(P("owner", None, None), P("owner", None), P()),
        check_vma=False,
    )
```

profile of v0, /device:TPU:1, one launch (start us, length us, event | category | flops | bytes accessed | tf_op | source)
XLA Modules:
  0.0 126.5 jit_solution(15650277266331991324)
XLA Ops:
  7.2 0.0 copy-start
  7.2 0.0 all-gather.2.cloned.1.call-start
  7.2 1.9 %abs_reduce_fusion = f32[2,1408]{1,0:T(2,128)S(1)} fusion(f32[2,1408,128]{2,1,0:T(8,128)} %param.3), kind=kLoop, calls=%fused_computation.1 | loop fusion | flops 718080 | bytes 1453056 | tf_op jit(solution)/shard_map/reduce_max | solution.py:28
  9.2 21.2 %all_to_all.10 = f32[16,2,1408]{2,1,0:T(2,128)S(1)} all-to-all(f32[16,2,1408]{2,1,0:T(2,128)S(1)} %broadcast_in_dim.8), channel_id=1, replica_groups=mesh['owner'=32,'rows'=16] {'rows'}, dimensions={0} | all-to-all | bytes 360448 | tf_op jit(solution)/shard_map/all_to_all | solution.py:9
  30.4 0.1 reduce_max.19
  30.5 0.0 copy-done
  30.5 0.0 copy-start.1
  30.5 0.0 copy-start.2
  30.5 0.0 copy-start.3
  30.5 1.3 %divide_convert_fusion = bf16[2,1408,128]{2,1,0:T(8,128)(2,1)} fusion(f32[2,1408,128]{2,1,0:T(8,128)S(1)} %copy-done, f32[2,1408]{1,0:T(2,128)S(1)} %reduce_max.19), kind=kLoop, calls=%fused_computation | loop fusion | flops 720896 | bytes 2173952 | tf_op jit(solution)/shard_map/convert_element_type | solution.py:29
  31.8 0.0 all-gather.2.cloned.1.call-update
  31.9 0.0 copy-done.1
  31.9 0.0 copy-done.2
  31.9 0.0 copy-done.3
  31.9 14.6 %all_gather.7 = bf16[2048,2]{0,1:T(2,128)(2,1)S(1)} all-gather(bf16[128,2]{0,1:T(2,128)(2,1)S(1)} %multiply_convert_fusion), channel_id=1, replica_groups=mesh['owner'=32,'rows'=16] {'rows'}, dimensions={0}, use_global_device_ids=true | all-gather | bytes 8704 | tf_op jit(solution)/shard_map/all_gather | solution.py:32
  46.5 0.1 broadcast_in_dim.9
  46.7 21.1 %all_to_all.11 = bf16[32,2048,2]{1,2,0:T(2,128)(2,1)S(1)} all-to-all(bf16[32,2048,2]{1,2,0:T(2,128)(2,1)S(1)} %broadcast_in_dim.9), channel_id=1, replica_groups=mesh['owner'=32,'rows'=16] {'owner'}, dimensions={0} | all-to-all | bytes 524288 | tf_op jit(solution)/shard_map/all_to_all | solution.py:9
  67.8 0.8 reshape.11
  68.6 40.9 %all-gather.2.cloned.1.call-done = bf16[2,1408,2048]{2,1,0:T(8,128)(2,1)} async-done(((bf16[2,1408,128]{2,1,0:T(8,128)(2,1)}), bf16[2,1408,2048]{2,1,0:T(8,128)(2,1)}) %all-gather.2.cloned.1.call-update) | async-done | bytes 11534352 | tf_op jit(solution)/shard_map/all_gather | solution.py:30
  109.5 10.1 %copy.9 = bf16[2,1408,2048]{2,1,0:T(8,128)(2,1)} copy(bf16[2,1408,2048]{2,1,0:T(8,128)(2,1)} %all-gather.2.cloned.1.call-done) | data formatting | bytes 23068672
  (2 shorter events, 0.1 us)
Async XLA Ops:
  7.2 23.3 %copy-start = (f32[2,1408,128]{2,1,0:T(8,128)S(1)}, f32[2,1408,128]{2,1,0:T(8,128)}, u32[]{:S(2)}) copy-start(f32[2,1408,128]{2,1,0:T(8,128)} %param.3) | copy-start | bytes 4325380
  7.2 102.4 %all-gather.2.cloned.1.call-start = ((), (), s32[]{:S(2)}) async-start(), calls=%async_computation.2 | async-start | bytes 12255232 | tf_op jit(solution)/shard_map/all_gather | solution.py:30
  30.5 1.4 %copy-start.1 = (f32[2,1408]{1,0:T(2,128)}, f32[2,1408]{1,0:T(2,128)S(1)}, u32[]{:S(2)}) copy-start(f32[2,1408]{1,0:T(2,128)S(1)} %reduce_max.19) | copy-start | bytes 33796
  30.5 1.4 %copy-start.2 = (f32[128,2]{0,1:T(2,128)S(1)}, f32[128,2]{0,1:T(2,128)}, u32[]{:S(2)}) copy-start(f32[128,2]{0,1:T(2,128)} %param.4) | copy-start | bytes 3076
  30.5 1.4 %copy-start.3 = (f32[128]{0:T(128)S(1)}, f32[128]{0:T(128)}, u32[]{:S(2)}) copy-start(f32[128]{0:T(128)} %param.5) | copy-start | bytes 1540
Sparse Core Ops, SparseCore 0:
  32.0 77.4 all-gather.1
where the time goes:
time: 127 us; the launch traced here: 126 us
  blocking collectives  57 us (45%)
  waiting for transfers between devices  41 us (32%)
  between operations  14.1 us (11%)
  local copies, waits for them, and re-layouts  11.1 us (9%)
  other arithmetic  3.29 us (3%)
    all_to_all x2, blocking collectives, sent_to_all(): return lax.all_to_all(copies, axis, split_axis=0, concat_axis=0, tiled=True)  42.3 us
    all_gather x1, waiting for transfers between devices, on_device(): serve_down = lax.all_gather(narrow_down, 'rows', axis=2, tiled=True)  40.9 us
    all_gather x1, blocking collectives, on_device(): row_router = lax.all_gather(part_router, 'rows', axis=0, tiled=True)  14.6 us
    unnamed x9, local copies, waits for them, and re-layouts  10.1 us
  transfers between devices with their start and end apart: 1, of which 1 were waited for; matrix products, arithmetic and copies ran while one was open for 1% of the time, Pallas kernels for 0%

commit v1 on v0

--- a/solution.py
+++ b/solution.py
@@ -27,7 +27,7 @@
 def on_device(w_down, router_weight, router_gain):
     scale_down = of_everyone(jnp.max(jnp.abs(w_down), axis=2), "rows")
     narrow_down = (w_down / jnp.expand_dims(scale_down, 2)).astype(jnp.bfloat16)
-    serve_down = lax.all_gather(narrow_down, "rows", axis=2, tiled=True)
+    serve_down = jnp.concatenate(lax.all_gather(narrow_down, "rows"), axis=2)
     part_router = (router_weight * router_gain[:, None]).astype(jnp.bfloat16)
     row_router = lax.all_gather(part_router, "rows", axis=0, tiled=True)
     serve_router = collect(row_router, "owner", 1)

time: 127 us -> 121 us (0.953)
  waiting for transfers between devices: 41 us -> 34.8 us
    reshape x0 -> x1, local copies, waits for them, and re-layouts: none -> 10.9 us  [on_device(): serve_down = jnp.concatenate(lax.all_gather(narrow_down, 'rows'), axis=2)]
    unnamed x9 -> x8, local copies, waits for them, and re-layouts: 10.1 us -> 0.02 us
    all_gather x1, waiting for transfers between devices: 40.9 us -> 34.8 us  [on_device(): serve_down = jnp.concatenate(lax.all_gather(narrow_down, 'rows'), axis=2)]
where the time goes in v1:
time: 121 us
  blocking collectives  57 us (47%)
  waiting for transfers between devices  34.8 us (29%)
  between operations  14.1 us (12%)
  local copies, waits for them, and re-layouts  12 us (10%)
  other arithmetic  3.29 us (3%)
    all_to_all x2, blocking collectives, sent_to_all(): return lax.all_to_all(copies, axis, split_axis=0, concat_axis=0, tiled=True)  42.3 us
    all_gather x1, waiting for transfers between devices, on_device(): serve_down = jnp.concatenate(lax.all_gather(narrow_down, 'rows'), axis=2)  34.8 us
    all_gather x1, blocking collectives, on_device(): row_router = lax.all_gather(part_router, 'rows', axis=0, tiled=True)  14.6 us
    reshape x1, local copies, waits for them, and re-layouts, on_device(): serve_down = jnp.concatenate(lax.all_gather(narrow_down, 'rows'), axis=2)  10.9 us
  transfers between devices with their start and end apart: 1, of which 1 were waited for; matrix products, arithmetic and copies ran while one was open for 1% of the time, Pallas kernels for 0%

profile of v1, /device:TPU:1, one launch (start us, length us, event | category | flops | bytes accessed | tf_op | source)
XLA Modules:
  0.0 121.2 jit_solution(7953694307968877948)
XLA Ops:
  7.2 0.0 copy-start
  7.2 0.0 all-gather.3.cloned.1.call-start
  7.2 1.9 %abs_reduce_fusion = f32[2,1408]{1,0:T(2,128)S(1)} fusion(f32[2,1408,128]{2,1,0:T(8,128)} %param.3), kind=kLoop, calls=%fused_computation.2 | loop fusion | flops 718080 | bytes 1453056 | tf_op jit(solution)/shard_map/reduce_max | solution.py:28
  9.2 21.2 %all_to_all.10 = f32[16,2,1408]{2,1,0:T(2,128)S(1)} all-to-all(f32[16,2,1408]{2,1,0:T(2,128)S(1)} %broadcast_in_dim.8), channel_id=1, replica_groups=mesh['owner'=32,'rows'=16] {'rows'}, dimensions={0} | all-to-all | bytes 360448 | tf_op jit(solution)/shard_map/all_to_all | solution.py:9
  30.4 0.1 reduce_max.19
  30.5 0.0 copy-done
  30.5 0.0 copy-start.1
  30.5 0.0 copy-start.2
  30.5 0.0 copy-start.3
  30.5 1.3 %divide_convert_fusion = bf16[2,1408,128]{2,1,0:T(8,128)(2,1)} fusion(f32[2,1408,128]{2,1,0:T(8,128)S(1)} %copy-done, f32[2,1408]{1,0:T(2,128)S(1)} %reduce_max.19), kind=kLoop, calls=%fused_computation.1 | loop fusion | flops 720896 | bytes 2173952 | tf_op jit(solution)/shard_map/convert_element_type | solution.py:29
  31.8 0.0 all-gather.3.cloned.1.call-update
  31.9 0.0 copy-done.1
  31.9 0.0 copy-done.2
  31.9 0.0 copy-done.3
  31.9 14.6 %all_gather.11 = bf16[2048,2]{0,1:T(2,128)(2,1)S(1)} all-gather(bf16[128,2]{0,1:T(2,128)(2,1)S(1)} %multiply_convert_fusion), channel_id=1, replica_groups=mesh['owner'=32,'rows'=16] {'rows'}, dimensions={0}, use_global_device_ids=true | all-gather | bytes 8704 | tf_op jit(solution)/shard_map/all_gather | solution.py:32
  46.5 0.1 broadcast_in_dim.9
  46.7 21.1 %all_to_all.11 = bf16[32,2048,2]{1,2,0:T(2,128)(2,1)S(1)} all-to-all(bf16[32,2048,2]{1,2,0:T(2,128)(2,1)S(1)} %broadcast_in_dim.9), channel_id=1, replica_groups=mesh['owner'=32,'rows'=16] {'owner'}, dimensions={0} | all-to-all | bytes 524288 | tf_op jit(solution)/shard_map/all_to_all | solution.py:9
  67.8 0.8 reshape.19
  68.6 34.8 %all-gather.3.cloned.1.call-done = bf16[32,1408,128]{2,1,0:T(8,128)(2,1)} async-done(((bf16[2,1408,128]{2,1,0:T(8,128)(2,1)}), bf16[32,1408,128]{2,1,0:T(8,128)(2,1)}) %all-gather.3.cloned.1.call-update) | async-done | bytes 11534352 | tf_op jit(solution)/shard_map/all_gather | solution.py:30
  103.4 10.9 %copy.14 = bf16[16,2,176,8,128]{4,3,0,2,1:T(8,128)(2,1)} copy(bf16[16,2,176,8,128]{4,3,2,1,0:T(8,128)(2,1)} %bitcast.10) | data formatting | bytes 23068672 | tf_op jit(solution)/shard_map/reshape | solution.py:30
  (2 shorter events, 0.1 us)
Async XLA Ops:
  7.2 23.3 %copy-start = (f32[2,1408,128]{2,1,0:T(8,128)S(1)}, f32[2,1408,128]{2,1,0:T(8,128)}, u32[]{:S(2)}) copy-start(f32[2,1408,128]{2,1,0:T(8,128)} %param.3) | copy-start | bytes 4325380
  7.2 96.2 %all-gather.3.cloned.1.call-start = ((), (), s32[]{:S(2)}) async-start(), calls=%async_computation.2 | async-start | bytes 12255232 | tf_op jit(solution)/shard_map/all_gather | solution.py:30
  30.5 1.4 %copy-start.1 = (f32[2,1408]{1,0:T(2,128)}, f32[2,1408]{1,0:T(2,128)S(1)}, u32[]{:S(2)}) copy-start(f32[2,1408]{1,0:T(2,128)S(1)} %reduce_max.19) | copy-start | bytes 33796
  30.5 1.4 %copy-start.2 = (f32[128,2]{0,1:T(2,128)S(1)}, f32[128,2]{0,1:T(2,128)}, u32[]{:S(2)}) copy-start(f32[128,2]{0,1:T(2,128)} %param.4) | copy-start | bytes 3076
  30.5 1.4 %copy-start.3 = (f32[128]{0:T(128)S(1)}, f32[128]{0:T(128)}, u32[]{:S(2)}) copy-start(f32[128]{0:T(128)} %param.5) | copy-start | bytes 1540
Sparse Core Ops, SparseCore 0:
  32.0 71.3 all-gather.2
